TPU v7x, 512 devices: a whole 4x8x8 slice. The times are simulated.
512 devices in a mesh: ra: 128 (over x_lo, y, z), dec: 4 (over x_hi, core).
Axes of the slice: x: 4 (x_hi: 2, x_lo: 2; x = x_hi * 2 + x_lo), y: 8, z: 8, core: 2. Of those that a mesh axis runs over, the one named last changes fastest.
Arguments:
- exposures: float32 [2, 1280, 49152], P(None, 'dec', 'ra'), may hold values from -6 to 6
- inv_variance: float32 [2, 1280, 49152], P(None, 'dec', 'ra'), may hold values from 0.25 to 4
- pixel_valid: int32 [2, 1280, 49152], P(None, 'dec', 'ra'), may hold values 0 or 1
- correlation: int32 [4, 128, 2], P('dec', 'ra'), may hold values 0 or 1
- pixel_offset: int32 [4, 128, 2, 2], P('dec', 'ra'), may hold values from -3 to 3
- subpixel: float32 [4, 128, 2, 2], P('dec', 'ra'), may hold values from -0.5 to 0.5
- psf_match: bfloat16 [63, 63], replicated, may hold values from -0.09375 to 0.09375
Outputs:
- matched: float32 [768, 32768], P('dec', 'ra')
- weight_map: float32 [768, 32768], P('dec', 'ra')
All inputs are finite; a program needn't handle non-finite values. No bound on the sum of `pixel_valid` or of `correlation` on one device may be relied on, other than what follows from the above.
Results may differ from a plain program's by a relative error of at most 0.007.
Values may be sent and summed in bfloat16 or wider, within the bound.
No kernel may reach another device: no remote copies, remote signals or barrier semaphores. Data moves between devices by JAX's collectives and lax.ppermute only.
A program may use at most 128 MiB of HBM per device.

v0:
```python
import jax
import jax.numpy as jnp
from jax import lax
from jax.experimental import pallas as pl
from jax.experimental.pallas import tpu as pltpu
from jax.sharding import PartitionSpec as P


ROWS = 192
COLS = 256
PROWS = 320
PCOLS = 384
BAND = 96
EXT = 256
HALF = 31
SIDE = 63
LEFT = 64 - HALF
TILES_K = 33
PI = 3.141592653589793
F32 = jnp.float32
BF16 = jnp.bfloat16


def swap_pairs(block, axis, firsts, wrap):
    count = lax.axis_size(axis)
    lows = [i for i in range(count) if firsts(i) and (wrap or i + 1 < count)]
    if not lows:
        return jnp.zeros_like(block)
    pairs = [(i, (i + 1) % count) for i in lows]
    return lax.ppermute(block, axis, pairs + [(b, a) for a, b in pairs])


def gather_pairs(block, axis):
    count = lax.axis_size(axis)
    groups = [[i, i + 1] for i in range(0, count, 2)]
    return lax.all_gather(block, axis, axis_index_groups=groups)


def is_odd(axis):
    return (lax.axis_index(axis) & 1) == 1


def sin_pi(z):
    y = z * PI
    y2 = y * y
    poly = 1.0 / 6227020800.0
    for factorial in (-39916800.0, 362880.0, -5040.0, 120.0, -6.0, 1.0):
        poly = poly * y2 + 1.0 / factorial
    return y * poly


def lanczos_map(offset, fraction, direction):
    lane = lax.broadcasted_iota(jnp.int32, (8, 128), 1)
    signed = jnp.where(lane < 64, lane, lane - 128) * direction
    step = signed + offset
    where_at = step.astype(F32) + fraction
    parity = 1.0 - 2.0 * (step & 1).astype(F32)
    frac = jnp.full((8, 128), fraction, F32)
    third = jnp.abs(where_at) * (1.0 / 3.0)
    folded = jnp.where(third > 0.5, 1.0 - third, third)
    safe = jnp.where(where_at == 0.0, 1.0, where_at)
    first = parity * sin_pi(frac) / (safe * PI)
    second = sin_pi(folded) * 3.0 / (jnp.abs(safe) * PI)
    value = jnp.where(where_at == 0.0, 1.0, first * second)
    value = jnp.where(jnp.abs(where_at) < 3.0, value, 0.0)
    rows = jnp.broadcast_to(value[0:1], (128, 128))
    turned = pltpu.roll(rows, 0, 1, stride=1, stride_axis=0)
    down = lax.broadcasted_iota(jnp.int32, (128, 128), 0)
    across = lax.broadcasted_iota(jnp.int32, (128, 128), 1)
    gap = across - down
    diagonal = jnp.where(jnp.abs(gap) <= 64, turned, 0.0)
    upper = jnp.where(gap < -64, turned, 0.0)
    lower = jnp.where(gap > 64, turned, 0.0)
    return diagonal, upper, lower


def row_map(offset, fraction):
    return jnp.concatenate(split(lanczos_map(offset, fraction, -1)[0]), axis=1)


def col_map(offset, fraction):
    diagonal, upper, lower = lanczos_map(offset, fraction, 1)
    return split(
        jnp.concatenate(
            [
                jnp.concatenate([diagonal, upper], axis=1),
                jnp.concatenate([lower, diagonal], axis=1),
            ],
            axis=0,
        )
    )


def split(value):
    high = value.astype(BF16)
    return high, (value - high.astype(F32)).astype(BF16)


def dot(a, b):
    return lax.dot_general(a, b, (((1,), (0,)), ((), ())), preferred_element_type=F32)


def joined(left, right):
    lane = lax.broadcasted_iota(jnp.int32, left[:, :128].shape, 1)
    middle = jnp.where(lane < 64, left[:, 128:], right[:, :128])
    return jnp.concatenate([left[:, :128], middle, right[:, 128:]], axis=1)


def warp_cols(half, pair):
    return [
        [
            dot(half[:, at : at + 256], pair[0]) + dot(half[:, at : at + 256], pair[1])
            for at in (PCOLS * n, PCOLS * n + 128)
        ]
        for n in range(2)
    ]


def added(first, second):
    return [joined(*(a + b for a, b in zip(first[n], second[n]))) for n in range(2)]


def warp_kernel(
    off_hbm, sub_hbm, cov_hbm, exp_hbm, inv_hbm, val_hbm,
    own, near, far, middle, row_maps, col_maps,
    off, sub, cov, exp, inv, val, small, large,
):
    scalars = [
        pltpu.make_async_copy(source, target, small.at[i])
        for i, (source, target) in enumerate(((off_hbm, off), (sub_hbm, sub), (cov_hbm, cov)))
    ]
    pieces = ((0, 320),)
    images = [
        [
            [
                pltpu.make_async_copy(
                    source.at[e, pl.ds(at, size)], target.at[e, pl.ds(at, size)], large.at[e, p, i]
                )
                for i, (source, target) in enumerate(((inv_hbm, inv), (val_hbm, val), (exp_hbm, exp)))
            ]
            for p, (at, size) in enumerate(pieces)
        ]
        for e in range(2)
    ]
    order = [(0, 0), (1, 0)]
    for copy in scalars + [copy for e, p in order for copy in images[e][p]]:
        copy.start()

    def load(e, p):
        at, size = pieces[p]
        cut = pl.ds(at, size)
        for copy in images[e][p]:
            copy.wait()
        masked = inv[e, cut] * (val[e, cut].astype(F32) * cov[0, 0, e].astype(F32))
        return jnp.concatenate([masked * exp[e, cut], masked], axis=1).astype(BF16)

    for copy in scalars:
        copy.wait()
    rows = [row_map(off[0, 0, e, 0], sub[0, 0, e, 0]) for e in range(2)]
    cols = [col_map(off[0, 0, e, 1], sub[0, 0, e, 1]) for e in range(2)]
    sums = []
    for e in range(2):
        data = load(e, 0)
        middle[e] = data[80:256]
        parts = [
            dot(lhs, jnp.concatenate([data[at : at + 128]] * 2, axis=0))
            for lhs, at in ((rows[e][:96], 0), (rows[e][32:], 192))
        ]
        sums.append(warp_cols(jnp.concatenate(parts, axis=0).astype(BF16), cols[e]))
    for e in range(2):
        row_maps[e] = rows[e]
        col_maps[e, 0], col_maps[e, 1] = cols[e]
    odd = is_odd("dec")
    for n, whole in enumerate(added(*sums)):
        own[n, :64], own[n, 64:] = whole[32:96], whole[96:160]
        top, bottom = whole[:BAND], whole[BAND:]
        near[n] = jnp.where(odd, top, bottom).astype(BF16)
        far[n] = jnp.where(odd, bottom, top).astype(BF16)


def middle_kernel(middle, row_maps, col_maps, own):
    sums = []
    for e in range(2):
        parts = [
            dot(row_maps[e, low:high], jnp.concatenate([middle[e, at : at + 128]] * 2, axis=0))
            for low, high, at in ((16, 112, 0), (64, 96, 48))
        ]
        half = jnp.concatenate(parts, axis=0).astype(BF16)
        sums.append(warp_cols(half, (col_maps[e, 0], col_maps[e, 1])))
    own[0], own[1] = added(*sums)


def is_outer():
    strip = lax.axis_index("dec")
    return (strip == 0) | (strip == lax.axis_size("dec") - 1)


def dec_sum(own, mid, near, far, odd, n, block):
    cut = pl.ds(block * 128 if isinstance(block, int) else pl.multiple_of(block * 128, 128), 128)
    other = 1 - (lax.axis_index("dec") & 1)
    first, second = near[other, n, :, cut].astype(F32), far[n, :, cut].astype(F32)
    above, below = jnp.where(odd, first, second), jnp.where(odd, second, first)
    return jnp.concatenate(
        [
            own[n, :64, cut] + above[:64],
            mid[n, :32, cut] + above[64:],
            mid[n, 32:96, cut],
            mid[n, 96:, cut] + below[:32],
            own[n, 64:, cut] + below[32:],
        ],
        axis=0,
    )


def pack(planes):
    lane = lax.broadcasted_iota(jnp.int32, (128, 128), 1)
    groups = [plane[128 * i : 128 * i + 128] for plane in planes for i in range(2)]
    return jnp.concatenate(
        [
            jnp.where(lane < 96, groups[i], pltpu.roll(groups[3], 96 - 32 * i, 1))
            for i in range(3)
        ],
        axis=0,
    )


def unpack(packed):
    lane = lax.broadcasted_iota(jnp.int32, (128, 128), 1)
    groups = [packed[128 * i : 128 * i + 128] for i in range(3)]
    last = pltpu.roll(groups[0], 32, 1)
    last = jnp.where(lane < 32, last, pltpu.roll(groups[1], 64, 1))
    last = jnp.where(lane < 64, last, pltpu.roll(groups[2], 96, 1))
    groups.append(last)
    return [jnp.concatenate(groups[2 * n : 2 * n + 2], axis=0) for n in range(2)]


def edges_kernel(own, mid, near, far, one, two):
    odd = is_odd("dec")
    west = pack([dec_sum(own, mid, near, far, odd, n, 0) for n in range(2)])
    east = pack([pltpu.roll(dec_sum(own, mid, near, far, odd, n, 2), 96, 1) for n in range(2)])
    odd = is_odd("ra")
    one[...] = jnp.where(odd, west, east).astype(BF16)
    two[...] = jnp.where(odd, east, west).astype(BF16)


def psf_kernel(psf, weights, taps):
    down = lax.broadcasted_iota(jnp.int32, (SIDE, 128), 0)
    across = lax.broadcasted_iota(jnp.int32, (SIDE, 128), 1)
    reverse = jnp.where(((down + across) & 127) == 0, 1.0, 0.0).astype(BF16)
    taps[...] = jnp.zeros((80, 128), F32)
    taps[8 : 8 + SIDE] = dot(psf[...], reverse)
    lane = lax.broadcasted_iota(jnp.int32, (128, 128), 1)
    weights[0] = jnp.zeros((256, 128), BF16)
    weights[TILES_K] = jnp.zeros((256, 128), BF16)
    before = jnp.zeros((128, 128), F32)
    for q in range(64):
        here = jnp.broadcast_to(taps[8 + q : 9 + q], (128, 128))
        here = pltpu.roll(here, 0, 1, stride=1, stride_axis=0)
        prev = jnp.concatenate([before[64:], before[:64]], axis=0)
        weights[1 + q // 2, 128 * (q % 2) : 128 * (q % 2) + 128] = jnp.where(
            lane < 64, here, prev
        ).astype(BF16)
        before = here


def outer_fill_kernel(psf, middle, row_maps, col_maps, weights, own, taps):
    @pl.when(is_outer())
    def _():
        psf_kernel(psf, weights, taps)
        middle_kernel(middle, row_maps, col_maps, own)


def inner_fill_kernel(psf, middle, row_maps, col_maps, ready, ready_own, weights, own, taps):
    @pl.when(jnp.logical_not(is_outer()))
    def _():
        psf_kernel(psf, weights, taps)
        middle_kernel(middle, row_maps, col_maps, own)


def half_match(half, base, bands, weights, weight, windows, stage):
    lane = lax.broadcasted_iota(jnp.int32, (EXT, 128), 1)
    east = half == 1
    planes = []
    for n, band in enumerate(unpack(bands)):
        band = jnp.where(
            east, jnp.where(lane < 96, band, 0.0), jnp.where(lane >= 32, pltpu.roll(band, 32, 1), 0.0)
        )
        left, right = base(n)
        planes.append(
            jnp.concatenate(
                [left + jnp.where(east, 0.0, band), right + jnp.where(east, band, 0.0)], axis=1
            )
        )
    numer, denom = planes
    row = lax.broadcasted_iota(jnp.int32, (EXT, 256), 0) + (lax.axis_index("dec") * ROWS - 32)
    inside = (row >= 0) & (row < lax.axis_size("dec") * ROWS)
    coadd = jnp.where(inside, numer / jnp.maximum(denom, 1.0), 0.0).astype(BF16).astype(F32)
    weight(pltpu.roll(denom, 256 - 64, 1)[32 : 32 + ROWS, :128])
    for k in range(2):
        windows[k] = pltpu.roll(coadd, 256 - LEFT - 64 * k, 1)[:, :128]
    total = None
    for t in range(TILES_K):
        left = jnp.concatenate(
            [
                jnp.concatenate(
                    [windows[k, pl.ds(2 * t + s + 1, 48, stride=4), :] for k in range(2)], axis=0
                )
                for s in range(2)
            ],
            axis=1,
        ).astype(BF16)
        right = jnp.concatenate([weights[t + 1], weights[t]], axis=1)
        part = dot(left, right)
        total = part if total is None else total + part
    lane = lax.broadcasted_iota(jnp.int32, (48, 128), 1)
    for p in range(4):
        cut = slice(128 * (p // 2), 128 * (p // 2) + 128)
        low, high = total[:48, cut], total[48:, cut]
        if p % 2:
            low = pltpu.roll(low, 64, 1)
        else:
            high = pltpu.roll(high, 64, 1)
        stage[pl.ds(p, 48, stride=4), :] = jnp.where(lane < 64, low, high)


def first_kernel(own, mid, near, far, one, other, weights, out, weight_map, base, windows):
    def weight(value):
        weight_map[...] = value

    odd = is_odd("dec")

    def block(n, at):
        return dec_sum(own, mid, near, far, odd, n, at)

    half = 1 - (lax.axis_index("ra") & 1)
    for n in range(2):
        for i in range(2):
            base[n, i] = block(n, 1 - half + i)
    bands = one[...].astype(F32) + other[...].astype(F32)
    half_match(
        half, lambda n: (block(n, half), block(n, half + 1)), bands, weights, weight, windows, out
    )


def second_kernel(
    two, weights, ready, ready_weight, base,
    out, weight_map,
    windows, stage, stage_weight, sems,
):
    half = lax.axis_index("ra") & 1
    this, that = (pl.ds(pl.multiple_of(128 * x, 128), 128) for x in (half, 1 - half))
    copies = [
        pltpu.make_async_copy(source, target, sems.at[i])
        for i, (source, target) in enumerate(
            (
                (ready, out.at[:, that]),
                (ready_weight, weight_map.at[:, that]),
                (stage_weight, weight_map.at[:, this]),
                (stage, out.at[:, this]),
            )
        )
    ]
    copies[0].start()
    copies[1].start()

    def weight(value):
        stage_weight[...] = value
        copies[2].start()

    bands = two[...].astype(F32)
    half_match(
        half, lambda n: (base[n, 0], base[n, 1]), bands, weights, weight, windows, stage
    )
    copies[3].start()
    for copy in copies:
        copy.wait()


HBM = pl.BlockSpec(memory_space=pltpu.HBM)
VMEM = pl.BlockSpec(memory_space=pltpu.VMEM)


def call(body, ins, outs, scratch=(), flops=0, limit=16, space=None, aliases=None):
    return pl.pallas_call(
        body,
        in_specs=ins,
        out_specs=tuple(space or VMEM for _ in outs),
        out_shape=outs,
        scratch_shapes=scratch,
        input_output_aliases=aliases or {},
        cost_estimate=pl.CostEstimate(flops=flops, transcendentals=0, bytes_accessed=4_000_000),
        compiler_params=pltpu.CompilerParams(vmem_limit_bytes=limit * 1024 * 1024),
    )


def array(shape, kind):
    return jax.ShapeDtypeStruct(shape, kind)


def shards(exposures, inv_variance, pixel_valid, correlation, pixel_offset, subpixel, psf_match):
    own, near, far, middle, row_maps, col_maps = call(
        warp_kernel,
        [HBM] * 6,
        (
            array((2, 128, PCOLS), F32),
            array((2, BAND, PCOLS), BF16),
            array((2, BAND, PCOLS), BF16),
            array((2, 176, 2 * PCOLS), BF16),
            array((2, 128, 256), BF16),
            array((2, 2, 256, 256), BF16),
        ),
        scratch=[
            pltpu.SMEM((1, 1, 2, 2), jnp.int32),
            pltpu.SMEM((1, 1, 2, 2), F32),
            pltpu.SMEM((1, 1, 2), jnp.int32),
            pltpu.VMEM((2, PROWS, PCOLS), F32),
            pltpu.VMEM((2, PROWS, PCOLS), F32),
            pltpu.VMEM((2, PROWS, PCOLS), jnp.int32),
            pltpu.SemaphoreType.DMA((3,)),
            pltpu.SemaphoreType.DMA((2, 1, 3)),
        ],
        flops=3_000_000_000,
    )(
        *(
            pltpu.with_memory_space_constraint(x, pltpu.HBM)
            for x in (pixel_offset, subpixel, correlation, exposures, inv_variance, pixel_valid)
        )
    )
    filled = (array((TILES_K + 1, 256, 128), BF16), array((2, 128, PCOLS), F32))
    taps = [pltpu.VMEM((80, 128), F32)]
    far = swap_pairs(far, "dec", lambda i: i % 2 == 1, False)
    weights, mid = call(
        outer_fill_kernel, [VMEM] * 4, filled, taps, 3_000_000_000
    )(psf_match, middle, row_maps, col_maps)
    near = gather_pairs(near, "dec")
    weights, mid = call(
        inner_fill_kernel, [VMEM] * 6, filled, taps, 3_000_000_000, aliases={4: 0, 5: 1}
    )(psf_match, middle, row_maps, col_maps, weights, mid)
    one, two = call(
        edges_kernel,
        [VMEM] * 4,
        (array((384, 128), BF16), array((384, 128), BF16)),
        flops=1_000_000,
    )(own, mid, near, far)
    first = swap_pairs(one, "ra", lambda i: i % 8 in (0, 2, 4), True)
    two = swap_pairs(two, "ra", lambda i: i % 2 == 1, True)
    last = swap_pairs(one, "ra", lambda i: i % 8 == 6, True)
    windows = pltpu.VMEM((2, EXT, 128), F32)
    stage = pltpu.VMEM((ROWS, 128), F32)
    ready, ready_weight, base = call(
        first_kernel,
        [VMEM] * 7,
        (
            array((ROWS, 128), F32),
            array((ROWS, 128), F32),
            array((2, 2, EXT, 128), F32),
        ),
        scratch=[windows],
        flops=3_000_000_000,
    )(own, mid, near, far, first, last, weights)
    return call(
        second_kernel,
        [VMEM] * 5,
        (array((ROWS, COLS), F32), array((ROWS, COLS), F32)),
        scratch=[windows, stage, stage, pltpu.SemaphoreType.DMA((4,))],
        flops=3_000_000_000,
        space=HBM,
    )(two, weights, ready, ready_weight, base)


def solution(mesh):
    return jax.shard_map(
        shards,
        mesh=mesh,
        in_specs=(
            P(None, "dec", "ra"),
            P(None, "dec", "ra"),
            P(None, "dec", "ra"),
            P("dec", "ra", None),
            P("dec", "ra", None, None),
            P("dec", "ra", None, None),
            P(),
        ),
        out_specs=(P("dec", "ra"), P("dec", "ra")),
        check_vma=False,
    )
```

profile of v0, /device:TPU:1, one launch (start us, length us, event | category | flops | bytes accessed | tf_op | source)
XLA Modules:
  0.0 34.4 jit_solution(11812933063712040361)
XLA Ops:
  0.6 0.0 copy-start
  0.6 2.5 %shard_map.86 = (f32[2,128,384]{2,1,0:T(8,128)S(1)}, bf16[2,96,384]{2,1,0:T(8,128)(2,1)S(1)}, bf16[2,96,384]{2,1,0:T(8,128)(2,1)S(1)}, bf16[2,176,768]{2,1,0:T(8...) custom-call(s32[1,1,2,2]{3,2,1,0:T(2,128)} %off_hbm.1, f32[1,1,2,2]{3,2,1,0:T(2,128)} %sub_hbm.1, ...), custom_call_target="tpu_custom_call" | custom-call | flops 3000000000 | bytes 4000000 | tf_op jit(solution)/shard_map/pallas_call | solution.py:401
  3.2 6.0 %collective-permute-start = (bf16[2,96,384]{2,1,0:T(8,128)(2,1)S(1)}, bf16[2,96,384]{2,1,0:T(8,128)(2,1)S(1)}, u32[]{:S(2)}, u32[]{:S(2)}) collective-permute-start(bf16[2,96,384]{2,1,0:T(8,128)(2,1)S(1)} %get-tuple-element.25), channel_id=1, source_target_pairs={{1,2},{2,1},{5,6},{6,5},{9,10},{10,9},{13,14},{14,13},{17,18},{18,... | collective-permute-start | bytes 442376 | tf_op jit(solution)/shard_map/ppermute | solution.py:30
  9.2 0.0 copy-done
  9.2 0.8 %shard_map.88 = (bf16[34,256,128]{2,1,0:T(8,128)(2,1)S(1)}, f32[2,128,384]{2,1,0:T(8,128)S(1)}) custom-call(bf16[63,63]{1,0:T(8,128)(2,1)S(1)} %copy-done, bf16[2,176,768]{2,1,0:T(8,128)(2,1)S(1)} %get-tuple-element.18.middle, bf16[2,128,256]{2,1,0:T(8,128)(2,1)S(1)} %get-tuple-element.19.row_maps, ...), custom_call_target="tpu_custom_call", output_to_operand_aliasing={{0}: (4, {}), {1}: (5, {})} | custom-call | flops 3000000000 | bytes 4000000 | tf_op jit(solution)/shard_map/pallas_call | solution.py:436
  10.1 3.1 %all-gather = bf16[4,96,384]{2,1,0:T(8,128)(2,1)S(1)} all-gather(bf16[2,96,384]{2,1,0:T(8,128)(2,1)S(1)} %get-tuple-element.24), channel_id=2, replica_groups={{0,1},{2,3},{4,5},{6,7},{8,9},{10,11},{12,13},{14,15},{16,17},{18,19},{..., dimensions={0}, use_global_device_ids=true | all-gather | bytes 442368 | tf_op jit(solution)/shard_map/all_gather | solution.py:36
  13.2 0.0 collective-permute-done.far
  13.2 0.2 shard_map.89
  13.4 2.9 %collective-permute-start.2 = (bf16[384,128]{1,0:T(8,128)(2,1)S(1)}, bf16[384,128]{1,0:T(8,128)(2,1)S(1)}, u32[]{:S(2)}, u32[]{:S(2)}) collective-permute-start(bf16[384,128]{1,0:T(8,128)(2,1)S(1)} %get-tuple-element.28), channel_id=1, source_target_pairs={{0,4},{8,12},{16,20},{32,36},{40,44},{48,52},{64,68},{72,76},{80,8... | collective-permute-start | bytes 294920 | tf_op jit(solution)/shard_map/ppermute | solution.py:30
  16.3 0.7 %collective-permute-start.3 = (bf16[384,128]{1,0:T(8,128)(2,1)S(1)}, bf16[384,128]{1,0:T(8,128)(2,1)S(1)}, u32[]{:S(2)}, u32[]{:S(2)}) collective-permute-start(bf16[384,128]{1,0:T(8,128)(2,1)S(1)} %get-tuple-element.28), channel_id=1, source_target_pairs={{24,28},{56,60},{88,92},{120,124},{152,156},{184,188},{216,220},{2... | collective-permute-start | bytes 294920 | tf_op jit(solution)/shard_map/ppermute | solution.py:30
  17.0 12.5 %collective-permute-start.1 = (bf16[384,128]{1,0:T(8,128)(2,1)S(1)}, bf16[384,128]{1,0:T(8,128)(2,1)S(1)}, u32[]{:S(2)}, u32[]{:S(2)}) collective-permute-start(bf16[384,128]{1,0:T(8,128)(2,1)S(1)} %get-tuple-element.26), channel_id=1, source_target_pairs={{4,8},{12,16},{20,24},{28,32},{36,40},{44,48},{52,56},{60,64},{68,... | collective-permute-start | bytes 294920 | tf_op jit(solution)/shard_map/ppermute | solution.py:30
  29.6 0.0 collective-permute-done.2.one
  29.6 0.0 collective-permute-done.3.other
  29.6 1.2 %shard_map.90 = (f32[192,128]{1,0:T(8,128)S(1)}, f32[192,128]{1,0:T(8,128)S(1)}, f32[2,2,256,128]{3,2,1,0:T(8,128)S(1)}) custom-call(f32[2,128,384]{2,1,0:T(8,128)S(1)} %get-tuple-element.17.own, f32[2,128,384]{2,1,0:T(8,128)S(1)} %get-tuple-element.23.mid, bf16[2,2,96,384]{3,2,1,0:T(8,128)(2,1)S(1)} %bitcast.2, ...), custom_call_target="tpu_custom_call" | custom-call | flops 3000000000 | bytes 4000000 | tf_op jit(solution)/shard_map/pallas_call | solution.py:450
  30.8 1.8 %collective-permute-done.1.two = bf16[384,128]{1,0:T(8,128)(2,1)S(1)} collective-permute-done((bf16[384,128]{1,0:T(8,128)(2,1)S(1)}, bf16[384,128]{1,0:T(8,128)(2,1)S(1)}, u32[]{:S(2)}, u32[]{:S(2)}) %collective-permute-start.1) | collective-permute-done | bytes 98336 | tf_op jit(solution)/shard_map/ppermute | solution.py:30
  32.6 1.8 %shard_map.91 = (f32[192,256]{1,0:T(8,128)}, f32[192,256]{1,0:T(8,128)}) custom-call(bf16[384,128]{1,0:T(8,128)(2,1)S(1)} %collective-permute-done.1.two, bf16[34,256,128]{2,1,0:T(8,128)(2,1)S(1)} %get-tuple-element.27.weights, f32[192,128]{1,0:T(8,128)S(1)} %get-tuple-element.29.ready, f32[192,128]{1,0:T(8,128)S(1)} %get-tuple-element.30.ready_weight, ...), custom_call_target="tpu_custom_call" | custom-call | flops 3000000000 | bytes 4000000 | tf_op jit(solution)/shard_map/pallas_call | solution.py:461
  (1 shorter events, 0.0 us)
Async XLA Ops:
  0.6 8.6 %copy-start = (bf16[63,63]{1,0:T(8,128)(2,1)S(1)}, bf16[63,63]{1,0:T(8,128)(2,1)}, u32[]{:S(2)}) copy-start(bf16[63,63]{1,0:T(8,128)(2,1)} %psf.3) | copy-start | bytes 23818
  3.2 10.0 %collective-permute-start = (bf16[2,96,384]{2,1,0:T(8,128)(2,1)S(1)}, bf16[2,96,384]{2,1,0:T(8,128)(2,1)S(1)}, u32[]{:S(2)}, u32[]{:S(2)}) collective-permute-start(bf16[2,96,384]{2,1,0:T(8,128)(2,1)S(1)} %get-tuple-element.25), channel_id=1, source_target_pairs={{1,2},{2,1},{5,6},{6,5},{9,10},{10,9},{13,14},{14,13},{17,18},{18,... | collective-permute-start | bytes 442376 | tf_op jit(solution)/shard_map/ppermute | solution.py:30
  13.4 16.1 %collective-permute-start.2 = (bf16[384,128]{1,0:T(8,128)(2,1)S(1)}, bf16[384,128]{1,0:T(8,128)(2,1)S(1)}, u32[]{:S(2)}, u32[]{:S(2)}) collective-permute-start(bf16[384,128]{1,0:T(8,128)(2,1)S(1)} %get-tuple-element.28), channel_id=1, source_target_pairs={{0,4},{8,12},{16,20},{32,36},{40,44},{48,52},{64,68},{72,76},{80,8... | collective-permute-start | bytes 294920 | tf_op jit(solution)/shard_map/ppermute | solution.py:30
  16.3 13.2 %collective-permute-start.3 = (bf16[384,128]{1,0:T(8,128)(2,1)S(1)}, bf16[384,128]{1,0:T(8,128)(2,1)S(1)}, u32[]{:S(2)}, u32[]{:S(2)}) collective-permute-start(bf16[384,128]{1,0:T(8,128)(2,1)S(1)} %get-tuple-element.28), channel_id=1, source_target_pairs={{24,28},{56,60},{88,92},{120,124},{152,156},{184,188},{216,220},{2... | collective-permute-start | bytes 294920 | tf_op jit(solution)/shard_map/ppermute | solution.py:30
  17.0 15.6 %collective-permute-start.1 = (bf16[384,128]{1,0:T(8,128)(2,1)S(1)}, bf16[384,128]{1,0:T(8,128)(2,1)S(1)}, u32[]{:S(2)}, u32[]{:S(2)}) collective-permute-start(bf16[384,128]{1,0:T(8,128)(2,1)S(1)} %get-tuple-element.26), channel_id=1, source_target_pairs={{4,8},{12,16},{20,24},{28,32},{36,40},{44,48},{52,56},{60,64},{68,... | collective-permute-start | bytes 294920 | tf_op jit(solution)/shard_map/ppermute | solution.py:30
where the time goes:
time: 34.6 us; the launch traced here: 34.4 us
  starting transfers between devices  22.1 us (64%)
  Pallas kernels  6.57 us (19%)
  blocking collectives  3.13 us (9%)
  waiting for transfers between devices  1.82 us (5%)
  between operations  0.74 us (2%)
    ppermute x4, starting transfers between devices, swap_pairs(): return lax.ppermute(block, axis, pairs + [(b, a) for a, b in pairs])  22.1 us
    all_gather x1, blocking collectives, gather_pairs(): return lax.all_gather(block, axis, axis_index_groups=groups)  3.13 us
    pallas_call x1, Pallas kernels, shards(): call(warp_kernel, [HBM] * 6, (array((2, 128, PCOLS), F32), array((2, BAND...  2.51 us
    ppermute x4, waiting for transfers between devices, swap_pairs(): return lax.ppermute(block, axis, pairs + [(b, a) for a, b in pairs])  1.82 us
    pallas_call x1, Pallas kernels, shards(): call(second_kernel, [VMEM] * 5, (array((ROWS, COLS), F32), array((ROWS, C...  1.8 us
    pallas_call x1, Pallas kernels, shards(): call(first_kernel, [VMEM] * 7, (array((ROWS, 128), F32), array((ROWS, 128...  1.18 us
    pallas_call x1, Pallas kernels, shards(): call(inner_fill_kernel, [VMEM] * 6, filled, taps, 3000000000, aliases={4:...  0.83 us
  transfers between devices with their start and end apart: 4, of which 1 were waited for; matrix products, arithmetic and copies ran while one was open for 0% of the time, Pallas kernels for 6%

commit v1 on v0

--- a/solution.py
+++ b/solution.py
@@ -278,13 +278,10 @@
 
 
 def half_match(half, base, bands, weights, weight, windows, stage):
-    lane = lax.broadcasted_iota(jnp.int32, (EXT, 128), 1)
     east = half == 1
     planes = []
     for n, band in enumerate(unpack(bands)):
-        band = jnp.where(
-            east, jnp.where(lane < 96, band, 0.0), jnp.where(lane >= 32, pltpu.roll(band, 32, 1), 0.0)
-        )
+        band = pltpu.roll(band, 32 * (1 - half), 1)
         left, right = base(n)
         planes.append(
             jnp.concatenate(

time: 34.6 us -> 34.6 us (level)
  no operation moved by 1% of the time
where the time goes in v1:
time: 34.6 us; the launch traced here: 34.4 us
  starting transfers between devices  22.1 us (64%)
  Pallas kernels  6.56 us (19%)
  blocking collectives  3.13 us (9%)
  waiting for transfers between devices  1.82 us (5%)
  between operations  0.74 us (2%)
    ppermute x4, starting transfers between devices, swap_pairs(): return lax.ppermute(block, axis, pairs + [(b, a) for a, b in pairs])  22.1 us
    all_gather x1, blocking collectives, gather_pairs(): return lax.all_gather(block, axis, axis_index_groups=groups)  3.13 us
    pallas_call x1, Pallas kernels, shards(): call(warp_kernel, [HBM] * 6, (array((2, 128, PCOLS), F32), array((2, BAND...  2.51 us
    ppermute x4, waiting for transfers between devices, swap_pairs(): return lax.ppermute(block, axis, pairs + [(b, a) for a, b in pairs])  1.82 us
    pallas_call x1, Pallas kernels, shards(): call(second_kernel, [VMEM] * 5, (array((ROWS, COLS), F32), array((ROWS, C...  1.8 us
    pallas_call x1, Pallas kernels, shards(): call(first_kernel, [VMEM] * 7, (array((ROWS, 128), F32), array((ROWS, 128...  1.18 us
    pallas_call x1, Pallas kernels, shards(): call(inner_fill_kernel, [VMEM] * 6, filled, taps, 3000000000, aliases={4:...  0.83 us
  transfers between devices with their start and end apart: 4, of which 1 were waited for; matrix products, arithmetic and copies ran while one was open for 0% of the time, Pallas kernels for 6%

profile of v1, /device:TPU:1, one launch (start us, length us, event | category | flops | bytes accessed | tf_op | source)
XLA Modules:
  0.0 34.4 jit_solution(4834805689962025069)
XLA Ops:
  0.6 0.0 copy-start
  0.6 2.5 %shard_map.86 = (f32[2,128,384]{2,1,0:T(8,128)S(1)}, bf16[2,96,384]{2,1,0:T(8,128)(2,1)S(1)}, bf16[2,96,384]{2,1,0:T(8,128)(2,1)S(1)}, bf16[2,176,768]{2,1,0:T(8...) custom-call(s32[1,1,2,2]{3,2,1,0:T(2,128)} %off_hbm.1, f32[1,1,2,2]{3,2,1,0:T(2,128)} %sub_hbm.1, ...), custom_call_target="tpu_custom_call" | custom-call | flops 3000000000 | bytes 4000000 | tf_op jit(solution)/shard_map/pallas_call | solution.py:398
  3.2 6.0 %collective-permute-start = (bf16[2,96,384]{2,1,0:T(8,128)(2,1)S(1)}, bf16[2,96,384]{2,1,0:T(8,128)(2,1)S(1)}, u32[]{:S(2)}, u32[]{:S(2)}) collective-permute-start(bf16[2,96,384]{2,1,0:T(8,128)(2,1)S(1)} %get-tuple-element.25), channel_id=1, source_target_pairs={{1,2},{2,1},{5,6},{6,5},{9,10},{10,9},{13,14},{14,13},{17,18},{18,... | collective-permute-start | bytes 442376 | tf_op jit(solution)/shard_map/ppermute | solution.py:30
  9.2 0.0 copy-done
  9.2 0.8 %shard_map.88 = (bf16[34,256,128]{2,1,0:T(8,128)(2,1)S(1)}, f32[2,128,384]{2,1,0:T(8,128)S(1)}) custom-call(bf16[63,63]{1,0:T(8,128)(2,1)S(1)} %copy-done, bf16[2,176,768]{2,1,0:T(8,128)(2,1)S(1)} %get-tuple-element.18.middle, bf16[2,128,256]{2,1,0:T(8,128)(2,1)S(1)} %get-tuple-element.19.row_maps, ...), custom_call_target="tpu_custom_call", output_to_operand_aliasing={{0}: (4, {}), {1}: (5, {})} | custom-call | flops 3000000000 | bytes 4000000 | tf_op jit(solution)/shard_map/pallas_call | solution.py:433
  10.1 3.1 %all-gather = bf16[4,96,384]{2,1,0:T(8,128)(2,1)S(1)} all-gather(bf16[2,96,384]{2,1,0:T(8,128)(2,1)S(1)} %get-tuple-element.24), channel_id=2, replica_groups={{0,1},{2,3},{4,5},{6,7},{8,9},{10,11},{12,13},{14,15},{16,17},{18,19},{..., dimensions={0}, use_global_device_ids=true | all-gather | bytes 442368 | tf_op jit(solution)/shard_map/all_gather | solution.py:36
  13.2 0.0 collective-permute-done.far
  13.2 0.2 shard_map.89
  13.4 2.9 %collective-permute-start.2 = (bf16[384,128]{1,0:T(8,128)(2,1)S(1)}, bf16[384,128]{1,0:T(8,128)(2,1)S(1)}, u32[]{:S(2)}, u32[]{:S(2)}) collective-permute-start(bf16[384,128]{1,0:T(8,128)(2,1)S(1)} %get-tuple-element.28), channel_id=1, source_target_pairs={{0,4},{8,12},{16,20},{32,36},{40,44},{48,52},{64,68},{72,76},{80,8... | collective-permute-start | bytes 294920 | tf_op jit(solution)/shard_map/ppermute | solution.py:30
  16.3 0.7 %collective-permute-start.3 = (bf16[384,128]{1,0:T(8,128)(2,1)S(1)}, bf16[384,128]{1,0:T(8,128)(2,1)S(1)}, u32[]{:S(2)}, u32[]{:S(2)}) collective-permute-start(bf16[384,128]{1,0:T(8,128)(2,1)S(1)} %get-tuple-element.28), channel_id=1, source_target_pairs={{24,28},{56,60},{88,92},{120,124},{152,156},{184,188},{216,220},{2... | collective-permute-start | bytes 294920 | tf_op jit(solution)/shard_map/ppermute | solution.py:30
  17.0 12.5 %collective-permute-start.1 = (bf16[384,128]{1,0:T(8,128)(2,1)S(1)}, bf16[384,128]{1,0:T(8,128)(2,1)S(1)}, u32[]{:S(2)}, u32[]{:S(2)}) collective-permute-start(bf16[384,128]{1,0:T(8,128)(2,1)S(1)} %get-tuple-element.26), channel_id=1, source_target_pairs={{4,8},{12,16},{20,24},{28,32},{36,40},{44,48},{52,56},{60,64},{68,... | collective-permute-start | bytes 294920 | tf_op jit(solution)/shard_map/ppermute | solution.py:30
  29.6 0.0 collective-permute-done.2.one
  29.6 0.0 collective-permute-done.3.other
  29.6 1.2 %shard_map.90 = (f32[192,128]{1,0:T(8,128)S(1)}, f32[192,128]{1,0:T(8,128)S(1)}, f32[2,2,256,128]{3,2,1,0:T(8,128)S(1)}) custom-call(f32[2,128,384]{2,1,0:T(8,128)S(1)} %get-tuple-element.17.own, f32[2,128,384]{2,1,0:T(8,128)S(1)} %get-tuple-element.23.mid, bf16[2,2,96,384]{3,2,1,0:T(8,128)(2,1)S(1)} %bitcast.2, ...), custom_call_target="tpu_custom_call" | custom-call | flops 3000000000 | bytes 4000000 | tf_op jit(solution)/shard_map/pallas_call | solution.py:447
  30.8 1.8 %collective-permute-done.1.two = bf16[384,128]{1,0:T(8,128)(2,1)S(1)} collective-permute-done((bf16[384,128]{1,0:T(8,128)(2,1)S(1)}, bf16[384,128]{1,0:T(8,128)(2,1)S(1)}, u32[]{:S(2)}, u32[]{:S(2)}) %collective-permute-start.1) | collective-permute-done | bytes 98336 | tf_op jit(solution)/shard_map/ppermute | solution.py:30
  32.6 1.8 %shard_map.91 = (f32[192,256]{1,0:T(8,128)}, f32[192,256]{1,0:T(8,128)}) custom-call(bf16[384,128]{1,0:T(8,128)(2,1)S(1)} %collective-permute-done.1.two, bf16[34,256,128]{2,1,0:T(8,128)(2,1)S(1)} %get-tuple-element.27.weights, f32[192,128]{1,0:T(8,128)S(1)} %get-tuple-element.29.ready, f32[192,128]{1,0:T(8,128)S(1)} %get-tuple-element.30.ready_weight, ...), custom_call_target="tpu_custom_call" | custom-call | flops 3000000000 | bytes 4000000 | tf_op jit(solution)/shard_map/pallas_call | solution.py:458
  (1 shorter events, 0.0 us)
Async XLA Ops:
  0.6 8.6 %copy-start = (bf16[63,63]{1,0:T(8,128)(2,1)S(1)}, bf16[63,63]{1,0:T(8,128)(2,1)}, u32[]{:S(2)}) copy-start(bf16[63,63]{1,0:T(8,128)(2,1)} %psf.3) | copy-start | bytes 23818
  3.2 10.0 %collective-permute-start = (bf16[2,96,384]{2,1,0:T(8,128)(2,1)S(1)}, bf16[2,96,384]{2,1,0:T(8,128)(2,1)S(1)}, u32[]{:S(2)}, u32[]{:S(2)}) collective-permute-start(bf16[2,96,384]{2,1,0:T(8,128)(2,1)S(1)} %get-tuple-element.25), channel_id=1, source_target_pairs={{1,2},{2,1},{5,6},{6,5},{9,10},{10,9},{13,14},{14,13},{17,18},{18,... | collective-permute-start | bytes 442376 | tf_op jit(solution)/shard_map/ppermute | solution.py:30
  13.4 16.1 %collective-permute-start.2 = (bf16[384,128]{1,0:T(8,128)(2,1)S(1)}, bf16[384,128]{1,0:T(8,128)(2,1)S(1)}, u32[]{:S(2)}, u32[]{:S(2)}) collective-permute-start(bf16[384,128]{1,0:T(8,128)(2,1)S(1)} %get-tuple-element.28), channel_id=1, source_target_pairs={{0,4},{8,12},{16,20},{32,36},{40,44},{48,52},{64,68},{72,76},{80,8... | collective-permute-start | bytes 294920 | tf_op jit(solution)/shard_map/ppermute | solution.py:30
  16.3 13.2 %collective-permute-start.3 = (bf16[384,128]{1,0:T(8,128)(2,1)S(1)}, bf16[384,128]{1,0:T(8,128)(2,1)S(1)}, u32[]{:S(2)}, u32[]{:S(2)}) collective-permute-start(bf16[384,128]{1,0:T(8,128)(2,1)S(1)} %get-tuple-element.28), channel_id=1, source_target_pairs={{24,28},{56,60},{88,92},{120,124},{152,156},{184,188},{216,220},{2... | collective-permute-start | bytes 294920 | tf_op jit(solution)/shard_map/ppermute | solution.py:30
  17.0 15.6 %collective-permute-start.1 = (bf16[384,128]{1,0:T(8,128)(2,1)S(1)}, bf16[384,128]{1,0:T(8,128)(2,1)S(1)}, u32[]{:S(2)}, u32[]{:S(2)}) collective-permute-start(bf16[384,128]{1,0:T(8,128)(2,1)S(1)} %get-tuple-element.26), channel_id=1, source_target_pairs={{4,8},{12,16},{20,24},{28,32},{36,40},{44,48},{52,56},{60,64},{68,... | collective-permute-start | bytes 294920 | tf_op jit(solution)/shard_map/ppermute | solution.py:30
